TPU v7x, 256 devices: a whole 4x4x8 slice. The times are simulated.
256 devices in a mesh: seq: 32 (over x, y, core), dp: 8 (over z).
Axes of the slice: x: 4, y: 4, z: 8, core: 2. Of those that a mesh axis runs over, the one named last changes fastest.
Arguments:
- queries: bfloat16 [16, 2048, 4096], P('dp', 'seq'), may hold values from -8 to 8
- unrotated_key_rows: bfloat16 [16, 2048, 1024], P('dp', 'seq'), may hold values from -8 to 8
- value_projection_rows: bfloat16 [16, 2048, 1024], P('dp', 'seq'), may hold values from -6 to 6
- attention_output_gradient: bfloat16 [16, 2048, 4096], P('dp', 'seq'), may hold values from -16 to 16
- normed_hidden_input: bfloat16 [16, 2048, 4096], P('dp', 'seq'), may hold values from -6 to 6
- adapter_down_weight: bfloat16 [4096, 64], replicated, may hold values from -0.01171875 to 0.01171875
- adapter_up_weight: bfloat16 [64, 4096], replicated, may hold values from -0.01171875 to 0.01171875
- lengths: int32 [16], P('dp'), may hold values from 1024 to 2048, as said below
- offsets: int32 [16], P('dp'), may hold values from 0 to 31
Outputs:
- grad_query: bfloat16 [16, 2048, 4096], P('dp', 'seq')
- grad_key: bfloat16 [16, 2048, 1024], P('dp', 'seq')
- grad_value: bfloat16 [16, 2048, 1024], P('dp', 'seq')
- grad_down: float32 [4096, 64], P('seq')
- grad_up: float32 [64, 4096], P(None, 'seq')
Inputs may be any that keep to these rules, and one draw needn't show every extreme that they name: `lengths`: in every draw at least one rollout has all 2048 positions valid.
All inputs are finite; a program needn't handle non-finite values.
Results may differ from a plain program's by a relative error of at most 0.018.
The roundings to bfloat16 on the way count: a program that leaves them out, or rounds other values in their place, can miss the bound.
Values may be sent and summed in bfloat16 or wider, within the bound.
No kernel may reach another device: no remote copies, remote signals or barrier semaphores. Data moves between devices by JAX's collectives and lax.ppermute only.
A program may use at most 64 MiB of HBM per device.

v0:
```python
from functools import partial

import jax
import jax.numpy as jnp
from jax import lax
from jax.sharding import PartitionSpec as P

HEAD_WIDTH = 128


rotary_base = 500000.0


def sent_together(arrays, axis, split_dim, concat_dim, along):
    ends, at = ([], 0)
    for a in arrays[:-1]:
        at += a.shape[along]
        ends.append(at)
    both = jnp.concatenate(arrays, axis=along)
    return tuple(
        jnp.split(
            lax.all_to_all(both, axis, split_axis=split_dim, concat_axis=concat_dim, tiled=True),
            ends,
            axis=along,
        )
    )


def in_blocks(x, dim, length):
    lengths = x.shape
    tiles = x.reshape(*lengths[:dim], length, lengths[dim] // length, *lengths[dim + 1 :])
    return jnp.moveaxis(tiles, dim, 0)


def sent_and_summed(x, axis, dim):
    length = lax.axis_size(axis)
    tiles = lax.all_to_all(in_blocks(x, dim, length), axis, 0, 0, tiled=True)
    return jnp.sum(tiles.astype(jnp.float32), axis=0)


def copy_for_each(x, axis):
    length = lax.axis_size(axis)
    return lax.all_to_all(jnp.broadcast_to(x[None], (length, *x.shape)), axis, 0, 0, tiled=True)


def taken_together(x, axis):
    everything = copy_for_each(x, axis)
    return jnp.sum(everything.astype(jnp.float32), axis=0)


def rotary_tables(length, head_size):
    half_size = head_size // 2
    frequency = rotary_base ** (-(jnp.arange(half_size, dtype=jnp.float32) * 2.0 / head_size))
    angles = jnp.arange(length, dtype=jnp.float32)[:, None] * frequency[None, :]
    return (jnp.cos(angles), jnp.sin(angles))


def rotate(fields, cosine, sine_table, direction):
    half_size = fields.shape[-1] // 2
    first_half = fields[..., :half_size]
    second_half = fields[..., half_size:]
    cos_wide = cosine[:, None, :]
    sin_wide = direction * sine_table[:, None, :]
    return jnp.concatenate(
        [
            first_half * cos_wide - second_half * sin_wide,
            second_half * cos_wide + first_half * sin_wide,
        ],
        axis=-1,
    )


def contract_axes(first_operand, second_operand, first_axis, second_axis):
    return lax.dot_general(
        first_operand,
        second_operand,
        (((first_axis,), (second_axis,)), ((), ())),
        preferred_element_type=jnp.float32,
    )


def block_terms(rot_query, rot_key, value_head, grad_head, offset, begin_row, end_row, score_scale):
    row_index = jnp.arange(begin_row, end_row, dtype=jnp.int32)[:, None]
    col_index = jnp.arange(end_row, dtype=jnp.int32)[None, :]
    visible = (col_index == row_index) | (col_index >= offset) & (col_index <= row_index)
    query_block = rot_query[begin_row:end_row]
    grad_block = grad_head[begin_row:end_row]
    key_block = rot_key[:end_row]
    value_block = value_head[:end_row]
    scores = contract_axes(query_block, key_block, 1, 1) * score_scale
    row_max = jnp.max(jnp.where(visible, scores, -jnp.inf), axis=1, keepdims=True)
    row_total = jnp.sum(jnp.where(visible, jnp.exp(scores - row_max), 0.0), axis=1, keepdims=True)
    grad_prob = contract_axes(grad_block, value_block, 1, 1)
    probability = jnp.where(visible, jnp.exp(scores - row_max), 0.0) / row_total
    row_delta = jnp.sum(probability * grad_prob, axis=1, keepdims=True)
    prob_low = probability.astype(jnp.bfloat16)
    grad_score = (probability * (grad_prob - row_delta) * score_scale).astype(jnp.bfloat16)
    block_grad = jnp.dot(grad_score, key_block, preferred_element_type=jnp.float32)
    key_add = contract_axes(grad_score, query_block, 0, 0)
    value_add = contract_axes(prob_low, grad_block, 0, 0)
    return (block_grad, key_add, value_add)


def head_backward(rot_query, rot_key, value_head, grad_head, offset, block_rows):
    length = rot_query.shape[0]
    head_size = rot_query.shape[1]
    score_scale = head_size ** (-0.5)
    query_parts = []
    key_terms = []
    value_terms = []
    for block_index in range(length // block_rows):
        begin_row = block_index * block_rows
        end_row = begin_row + block_rows
        live_terms = partial(
            block_terms,
            rot_query,
            rot_key,
            value_head,
            grad_head,
            offset,
            begin_row,
            end_row,
            score_scale,
        )
        results = live_terms()
        block_grad, key_add, value_add = results
        query_parts.append(block_grad)
        key_terms.append(jnp.pad(key_add, ((0, length - end_row), (0, 0))))
        value_terms.append(jnp.pad(value_add, ((0, length - end_row), (0, 0))))
    key_accum = key_terms[0]
    value_accum = value_terms[0]
    for term_index in range(1, len(key_terms)):
        key_accum = key_accum + key_terms[term_index]
        value_accum = value_accum + value_terms[term_index]
    return (jnp.concatenate(query_parts, axis=0), key_accum, value_accum)


def on_device(
    queries,
    unrotated_key_rows,
    value_projection_rows,
    attention_output_gradient,
    normed_hidden_input,
    adapter_down_weight,
    adapter_up_weight,
    lengths,
    offsets,
):
    rollout_count = queries.shape[0]
    tokens = queries.shape[1]
    seq_parts = lax.axis_size("seq")
    length = tokens * seq_parts
    query_width = queries.shape[2]
    head_count = query_width // HEAD_WIDTH
    key_groups = unrotated_key_rows.shape[2] // HEAD_WIDTH
    group_size = head_count // key_groups
    local_heads = head_count // seq_parts
    adapter_rank_size = adapter_down_weight.shape[1]
    query_tokens = queries.reshape(rollout_count, tokens, head_count, HEAD_WIDTH)
    grad_tokens = attention_output_gradient.reshape(rollout_count, tokens, head_count, HEAD_WIDTH)
    key_wide = jnp.repeat(
        unrotated_key_rows.reshape(rollout_count, tokens, key_groups, HEAD_WIDTH),
        group_size,
        axis=2,
    )
    value_wide = jnp.repeat(
        value_projection_rows.reshape(rollout_count, tokens, key_groups, HEAD_WIDTH),
        group_size,
        axis=2,
    )
    query_heads, key_heads, value_heads, grad_heads = sent_together(
        (query_tokens, key_wide, value_wide, grad_tokens), "seq", 2, 1, 0
    )
    cosine, sine_table = rotary_tables(length, HEAD_WIDTH)
    positions = jnp.arange(length, dtype=jnp.int32)
    keep_mask = (positions[None, :] >= offsets[:, None]) & (positions[None, :] < lengths[:, None])
    grad_heads = jnp.where(keep_mask[:, :, None, None], grad_heads, jnp.zeros_like(grad_heads))
    rot_query = rotate(query_heads.astype(jnp.float32), cosine, sine_table, 1.0).astype(
        jnp.bfloat16
    )
    rot_key = rotate(key_heads.astype(jnp.float32), cosine, sine_table, 1.0).astype(jnp.bfloat16)
    block_rows = min(512, length)
    query_rolls = []
    key_rolls = []
    value_rolls = []
    for rollout_slot in range(rollout_count):
        key_slot = 0 // local_heads
        query_grad, key_grad, value_grad = head_backward(
            rot_query[rollout_slot, :, 0],
            rot_key[rollout_slot, :, key_slot],
            value_heads[rollout_slot, :, key_slot],
            grad_heads[rollout_slot, :, 0],
            offsets[rollout_slot],
            block_rows,
        )
        query_list = [
            rotate(query_grad[:, None, :], cosine, sine_table, -1.0)[:, 0].astype(jnp.bfloat16)
        ]
        key_list = [
            rotate(key_grad[:, None, :], cosine, sine_table, -1.0)[:, 0].astype(jnp.bfloat16)
        ]
        value_list = [value_grad.astype(jnp.bfloat16)]
        query_rolls.append(jnp.stack(query_list, axis=1))
        key_rolls.append(jnp.stack(key_list, axis=1))
        value_rolls.append(jnp.stack(value_list, axis=1))
    query_back = jnp.stack(query_rolls, axis=0)
    key_parts = jnp.stack(key_rolls, axis=0)
    value_parts = jnp.stack(value_rolls, axis=0)
    query_result, key_result, value_result = sent_together(
        (query_back, key_parts, value_parts), "seq", 1, 2, 0
    )
    key_total = (
        key_result.astype(jnp.float32)
        .reshape(rollout_count, tokens, key_groups, group_size, HEAD_WIDTH)
        .sum(axis=3)
        .astype(jnp.bfloat16)
    )
    value_total = (
        value_result.astype(jnp.float32)
        .reshape(rollout_count, tokens, key_groups, group_size, HEAD_WIDTH)
        .sum(axis=3)
        .astype(jnp.bfloat16)
    )
    key_total = key_total.reshape(rollout_count, tokens, key_groups * HEAD_WIDTH)
    value_total = value_total.reshape(rollout_count, tokens, key_groups * HEAD_WIDTH)
    flattened_query = query_result.reshape(rollout_count * tokens, query_width)
    hidden_state = normed_hidden_input.reshape(rollout_count * tokens, normed_hidden_input.shape[2])
    adapter_latent = jnp.dot(
        hidden_state, adapter_down_weight, preferred_element_type=jnp.float32
    ).astype(jnp.bfloat16)
    backward_gradient = contract_axes(flattened_query, adapter_up_weight, 1, 1).astype(jnp.bfloat16)
    joined_terms = sent_and_summed(
        jnp.concatenate(
            [
                contract_axes(hidden_state, backward_gradient, 0, 0),
                contract_axes(flattened_query, adapter_latent, 0, 0),
            ],
            axis=1,
        ).astype(jnp.bfloat16),
        "seq",
        0,
    )
    down_local = joined_terms[:, :adapter_rank_size]
    up_local = joined_terms[:, adapter_rank_size:]
    down_sum, up_sum = (
        taken_together(down_local.astype(jnp.bfloat16), "dp").astype(jnp.float32),
        taken_together(up_local.astype(jnp.bfloat16), "dp").astype(jnp.float32),
    )
    return (
        flattened_query.reshape(rollout_count, tokens, query_width),
        key_total,
        value_total,
        down_sum,
        up_sum.T,
    )


def solution(mesh):
    in_specs = (
        P("dp", "seq", None),
        P("dp", "seq", None),
        P("dp", "seq", None),
        P("dp", "seq", None),
        P("dp", "seq", None),
        P(),
        P(),
        P("dp"),
        P("dp"),
    )
    out_specs = (
        P("dp", "seq", None),
        P("dp", "seq", None),
        P("dp", "seq", None),
        P("seq", None),
        P(None, "seq"),
    )
    return jax.shard_map(
        on_device, mesh=mesh, in_specs=in_specs, out_specs=out_specs, check_vma=False
    )
```

profile of v0, /device:TPU:2, one launch (start us, length us, event | category | flops | bytes accessed | tf_op | source)
XLA Modules:
  0.0 290.8 jit_solution(8194306516743843267)
XLA Ops:
  0.7 1.1 copy.150
  1.8 1.0 copy.151
  2.8 1.4 copy.149
  5.9 3.6 %copy.120 = bf16[8,64,32,128]{3,1,0,2:T(8,128)(2,1)} copy(bf16[8,64,32,128]{3,2,1,0:T(8,128)(2,1)S(1)} %pad_maximum_fusion) | data formatting | bytes 8388608 | tf_op jit(solution)/shard_map/concatenate | solution.py:19
  9.4 8.2 %all-to-all-start = ((bf16[8,64,32,128]{3,1,0,2:T(8,128)(2,1)}), bf16[8,64,32,128]{3,1,0,2:T(8,128)(2,1)}, u32[]{:S(2)}, u32[]{:S(2)}) async-start(bf16[8,64,32,128]{3,1,0,2:T(8,128)(2,1)} %copy.120), calls=%async_computation | async-start | bytes 8388608 | tf_op jit(solution)/shard_map/all_to_all | solution.py:22
  18.9 1.2 iota_compare_fusion.14
  20.6 1.8 iota_compare_fusion.12
  22.4 1.8 iota_compare_fusion.8
  24.2 1.8 iota_compare_fusion.9
  26.1 3.9 %fusion.47 = (f32[2048,64]{1,0:T(8,128)S(1)}, f32[2048,64]{1,0:T(8,128)S(1)}) fusion(f32[64]{0:T(128)S(1)} %negate_power_fusion), kind=kLoop, calls=%fused_computation.121 | loop fusion | flops 131072 | bytes 1048832 | tf_op jit(solution)/shard_map/cos | solution.py:55
  30.0 37.4 %all-to-all-done = bf16[8,64,32,128]{3,1,0,2:T(8,128)(2,1)} async-done(((bf16[8,64,32,128]{3,1,0,2:T(8,128)(2,1)}), bf16[8,64,32,128]{3,1,0,2:T(8,128)(2,1)}, u32[]{:S(2)}, u32[]{:S(2)}) %all-to-all-start) | async-done | bytes 4194336 | tf_op jit(solution)/shard_map/all_to_all | solution.py:22
  67.4 3.1 %copy.164 = bf16[8,64,32,128]{3,1,2,0:T(8,128)(2,1)S(1)} copy(bf16[8,64,32,128]{3,1,0,2:T(8,128)(2,1)} %all-to-all-done) | data formatting | bytes 8388608 | tf_op jit(solution)/shard_map/all_to_all | solution.py:22
  70.7 0.9 fusion.159
  71.6 0.7 fusion.158
  72.7 1.6 subtract_convert_fusion
  75.0 1.4 bitcast_select_fusion
  76.7 1.1 fusion.67
  80.0 1.1 fusion.65
  83.6 1.6 select_reduce_fusion.4
  85.2 2.6 fusion.37
  87.8 2.2 multiply_reduce_fusion.4
  90.1 1.3 fusion.41
  94.1 1.3 fusion.43
  95.4 1.7 select_reduce_fusion.2
  97.1 2.5 fusion.23
  99.6 2.6 fusion.30
  102.2 2.9 multiply_reduce_fusion.2
  105.1 2.7 fusion.32
  107.8 1.9 multiply_reduce_fusion.3
  109.7 3.5 %multiply_convert_fusion.2 = (bf16[512,1536]{1,0:T(8,128)(2,1)S(1)}, bf16[512,1536]{1,0:T(8,128)(2,1)S(1)}) fusion(f32[512,1536]{1,0:T(8,128)S(1)} %get-tuple-element.76, f32[512]{0:T(512)S(1)} %get-tuple-element.9, f32[512]{0:T(512)S(1)} %get-tuple-element.11, f32[512,1536]{1,0:T(8,128)S(1)} %get-tuple-element.74, f32[512]{0:T(512)S(1)} %get-tuple-element.73, ...), kind=kLoop, calls=%fused_computation.19 | loop fusion | flops 15728640 | bytes 15746048 | tf_op jit(solution)/shard_map/convert_element_type | solution.py:97
  113.2 1.4 fusion.122
  115.3 1.4 fusion.121
  117.3 1.9 select_reduce_fusion
  119.3 3.6 %fusion.11 = (f32[512]{0:T(512)S(1)}, f32[512]{0:T(512)S(1)}, f32[512,2048]{1,0:T(8,128)S(1)}) fusion(f32[512,2048]{1,0:T(8,128)S(1)} %get-tuple-element.68, f32[512]{0:T(512)S(1)} %get-tuple-element.67, pred[2048]{0:T(1024)(128)(4,1)S(1)} %copy-done.12, s32[512]{0:T(512)S(1)} %copy-done.11, pred[2048]{0:T(1024)(128)(4,1)S(1)} %copy-done.13, ...), kind=kOutput, calls=%fused_computation.36 | convolution fusion | flops 283376640 | bytes 10498048 | tf_op jit(solution)/shard_map/dot_general | solution.py:74
  122.9 4.4 %multiply_reduce_fusion = (f32[512]{0:T(512)}, f32[512]{0:T(512)S(1)}, f32[512,2048]{1,0:T(8,128)S(1)}) fusion(f32[512]{0:T(512)S(1)} %get-tuple-element.15, f32[512]{0:T(512)S(1)} %get-tuple-element.67, f32[512,2048]{1,0:T(8,128)S(1)} %get-tuple-element.68, pred[2048]{0:T(1024)(128)(4,1)S(1)} %copy-done.12, s32[512]{0:T(512)S(1)} %copy-done.11, ...), kind=kOutput, calls=%fused_computation.4 | convolution fusion | flops 285211648 | bytes 13254656 | tf_op jit(solution)/shard_map/dot_general | solution.py:74
  127.3 3.5 %multiply_reduce_fusion.1 = (f32[512]{0:T(512)}, f32[512,2048]{1,0:T(8,128)S(1)}) fusion(f32[512]{0:T(512)S(1)} %get-tuple-element.14, f32[512]{0:T(512)S(1)} %get-tuple-element.16, f32[512,2048]{1,0:T(8,128)S(1)} %get-tuple-element.69, pred[2048]{0:T(1024)(128)(4,1)S(1)} %copy-done.13, s32[512]{0:T(512)S(1)} %copy-done.11, ...), kind=kOutput, calls=%fused_computation.8 | convolution fusion | flops 278920704 | bytes 9054208 | tf_op jit(solution)/shard_map/dot_general | solution.py:74
  130.9 5.8 %multiply_convert_fusion = (bf16[512,2048]{1,0:T(8,128)(2,1)S(1)}, bf16[512,2048]{1,0:T(8,128)(2,1)S(1)}) fusion(f32[512,2048]{1,0:T(8,128)S(1)} %get-tuple-element.70, f32[512]{0:T(512)} %get-tuple-element.13, f32[512]{0:T(512)} %copy-done.20, f32[512]{0:T(512)} %copy-done.18, f32[512,2048]{1,0:T(8,128)S(1)} %get-tuple-element.68, ...), kind=kLoop, calls=%fused_computation.3 | loop fusion | flops 23068672 | bytes 20989952 | tf_op jit(solution)/shard_map/convert_element_type | solution.py:97
  136.7 0.8 fusion.120
  137.5 0.7 fusion.163
  138.2 0.8 fusion.13
  139.0 0.7 fusion.12
  140.6 5.4 %subtract_convert_fusion.2 = (bf16[2048,1,64]{2,0,1:T(8,128)(2,1)S(1)}, bf16[2048,1,64]{2,0,1:T(8,128)(2,1)S(1)}, bf16[2048,1,64]{2,0,1:T(8,128)(2,1)S(1)}, bf16...) fusion(f32[2048,1,128]{2,0,1:T(8,128)S(1)} %fusion.12, ...), kind=kLoop, calls=%fused_computation.101 | loop fusion | flops 4456448 | bytes 6291712 | tf_op jit(solution)/shard_map/convert.10
  147.7 2.8 fusion.19
  150.5 2.8 fusion.17
  153.3 12.1 %copy.130 = bf16[6,2048,1,128]{3,0,2,1:T(8,128)(2,1)S(1)} copy(bf16[6,2048,1,128]{3,1,2,0:T(8,128)(2,1)S(1)} %fusion.17) | data formatting | bytes 6291456 | tf_op jit(solution)/shard_map/concatenate | solution.py:19
  165.4 57.1 %all_to_all.45 = bf16[6,2048,1,128]{3,0,2,1:T(8,128)(2,1)S(1)} all-to-all(bf16[6,2048,1,128]{3,0,2,1:T(8,128)(2,1)S(1)} %copy.130), channel_id=1, replica_groups=mesh['seq'=32,'dp'=8] {'seq'}, dimensions={1} | all-to-all | bytes 6291456 | tf_op jit(solution)/shard_map/all_to_all | solution.py:22
  222.9 2.0 fusion.160
  225.6 1.5 copy.165
  227.1 1.0 fusion.38
  228.1 0.9 copy.166
  229.0 1.6 copy.136
  230.6 3.2 %convolution_convert_fusion.1 = bf16[32,128,64]{1,2,0:T(8,128)(2,1)} fusion(bf16[32,128,128]{2,1,0:T(8,128)(2,1)S(1)} %bitcast.300, bf16[128,4096]{1,0:T(8,128)(2,1)S(1)} %bitcast.291, bf16[4096,64]{0,1:T(8,128)(2,1)} %param.14), kind=kOutput, calls=%fused_computation.83 | convolution fusion | flops 134488064 | bytes 3145728 | tf_op jit(solution)/shard_map/dot_general | solution.py:74
  233.8 2.3 pad_maximum_fusion.1
  236.2 6.4 %all-to-all-start.2 = ((bf16[32,128,128]{1,2,0:T(8,128)(2,1)}), bf16[32,128,128]{1,2,0:T(8,128)(2,1)S(1)}, u32[]{:S(2)}, u32[]{:S(2)}) async-start(bf16[32,128,128]{1,2,0:T(8,128)(2,1)} %pad_maximum_fusion.1), calls=%async_computation.2 | async-start | bytes 2097152 | tf_op jit(solution)/shard_map/all_to_all | solution.py:37
  242.6 2.2 reduce.1
  244.8 1.4 reduce
  246.2 10.8 %all-to-all-done.2 = bf16[32,128,128]{1,2,0:T(8,128)(2,1)S(1)} async-done(((bf16[32,128,128]{1,2,0:T(8,128)(2,1)}), bf16[32,128,128]{1,2,0:T(8,128)(2,1)S(1)}, u32[]{:S(2)}, u32[]{:S(2)}) %all-to-all-start.2) | async-done | bytes 1048608 | tf_op jit(solution)/shard_map/all_to_all | solution.py:37
  257.9 8.5 %all-to-all-start.4 = ((bf16[8,128,64]{1,2,0:T(8,128)(2,1)}), bf16[8,128,64]{1,2,0:T(8,128)(2,1)S(1)}, u32[]{:S(2)}, u32[]{:S(2)}) async-start(bf16[8,128,64]{1,2,0:T(8,128)(2,1)} %broadcast_in_dim.157), calls=%async_computation.4 | async-start | bytes 262144 | tf_op jit(solution)/shard_map/all_to_all | solution.py:43
  266.3 1.7 copy_bitcast_fusion.2
  268.0 8.4 %all-to-all-done.4 = bf16[8,128,64]{1,2,0:T(8,128)(2,1)S(1)} async-done(((bf16[8,128,64]{1,2,0:T(8,128)(2,1)}), bf16[8,128,64]{1,2,0:T(8,128)(2,1)S(1)}, u32[]{:S(2)}, u32[]{:S(2)}) %all-to-all-start.4) | async-done | bytes 131104 | tf_op jit(solution)/shard_map/all_to_all | solution.py:43
  277.1 3.4 %all-to-all-start.3 = ((bf16[8,128,64]{1,2,0:T(8,128)(2,1)}), bf16[8,128,64]{1,2,0:T(8,128)(2,1)S(1)}, u32[]{:S(2)}, u32[]{:S(2)}) async-start(bf16[8,128,64]{1,2,0:T(8,128)(2,1)} %broadcast_in_dim.156), calls=%async_computation.3 | async-start | bytes 262144 | tf_op jit(solution)/shard_map/all_to_all | solution.py:43
  280.5 0.7 copy_bitcast_fusion.3
  281.2 1.3 reshape_reshape.3
  283.1 6.8 %all-to-all-done.3 = bf16[8,128,64]{1,2,0:T(8,128)(2,1)S(1)} async-done(((bf16[8,128,64]{1,2,0:T(8,128)(2,1)}), bf16[8,128,64]{1,2,0:T(8,128)(2,1)S(1)}, u32[]{:S(2)}, u32[]{:S(2)}) %all-to-all-start.3) | async-done | bytes 131104 | tf_op jit(solution)/shard_map/all_to_all | solution.py:43
  (119 shorter events, 19.8 us)
Async XLA Ops:
  0.6 226.5 %copy-start = (bf16[2,64,4096]{2,1,0:T(8,128)(2,1)S(1)}, bf16[2,64,4096]{2,1,0:T(8,128)(2,1)}, u32[]{:S(2)}) copy-start(bf16[2,64,4096]{2,1,0:T(8,128)(2,1)} %param.13) | copy-start | bytes 3145732
  0.6 3.6 %copy-start.1 = (bf16[2,64,4096]{2,1,0:T(8,128)(2,1)S(1)}, bf16[2,64,4096]{2,1,0:T(8,128)(2,1)}, u32[]{:S(2)}) copy-start(bf16[2,64,4096]{2,1,0:T(8,128)(2,1)} %param.12) | copy-start | bytes 3145732
  9.4 8.2 %copy-start.17 = (s32[2]{0:T(128)S(1)}, s32[2]{0:T(128)}, u32[]{:S(2)}) copy-start(s32[2]{0:T(128)} %param.17) | copy-start | bytes 28
  9.4 16.6 %copy-start.28 = (s32[2]{0:T(128)S(1)}, s32[2]{0:T(128)}, u32[]{:S(2)}) copy-start(s32[2]{0:T(128)} %param.16) | copy-start | bytes 28
  9.4 57.9 %all-to-all-start = ((bf16[8,64,32,128]{3,1,0,2:T(8,128)(2,1)}), bf16[8,64,32,128]{3,1,0,2:T(8,128)(2,1)}, u32[]{:S(2)}, u32[]{:S(2)}) async-start(bf16[8,64,32,128]{3,1,0,2:T(8,128)(2,1)} %copy.120), calls=%async_computation | async-start | bytes 8388608 | tf_op jit(solution)/shard_map/all_to_all | solution.py:22
  17.7 52.9 %copy-start.26 = (f32[64]{0:T(128)}, f32[64]{0:T(128)S(1)}, u32[]{:S(2)}) copy-start(f32[64]{0:T(128)S(1)} %negate_power_fusion) | copy-start | bytes 772
  78.6 0.8 copy-start.16
  82.6 1.0 copy-start.9
  82.6 1.0 copy-start.10
  93.6 1.8 copy-start.8
  95.4 1.7 copy-start.15
  116.6 0.7 copy-start.11
  116.6 0.7 copy-start.12
  117.3 1.9 copy-start.13
  119.3 3.6 %copy-start.18 = (f32[512]{0:T(512)}, f32[512]{0:T(512)S(1)}, u32[]{:S(2)}) copy-start(f32[512]{0:T(512)S(1)} %get-tuple-element.67) | copy-start | bytes 6148
  122.9 4.5 %copy-start.20 = (f32[512]{0:T(512)}, f32[512]{0:T(512)S(1)}, u32[]{:S(2)}) copy-start(f32[512]{0:T(512)S(1)} %get-tuple-element.15) | copy-start | bytes 6148
  122.9 4.5 %copy-start.22 = (f32[512]{0:T(512)}, f32[512]{0:T(512)S(1)}, u32[]{:S(2)}) copy-start(f32[512]{0:T(512)S(1)} %get-tuple-element.16) | copy-start | bytes 6148
  122.9 4.4 %copy-start.5 = (bf16[1,32,64,1,128]{4,2,1,0,3:T(8,128)(2,1)S(1)}, bf16[1,32,64,1,128]{4,2,1,0,3:T(8,128)(2,1)}, u32[]{:S(2)}) copy-start(bf16[1,32,64,1,128]{4,2,1,0,3:T(8,128)(2,1)} %get-tuple-element.35) | copy-start | bytes 1572868
  127.3 3.5 %copy-start.24 = (f32[512]{0:T(512)}, f32[512]{0:T(512)S(1)}, u32[]{:S(2)}) copy-start(f32[512]{0:T(512)S(1)} %get-tuple-element.14) | copy-start | bytes 6148
  139.0 1.0 copy-start.3
  139.0 1.0 copy-start.2
  139.9 0.6 copy-start.27
  146.0 1.5 copy-start.7
  146.0 1.5 copy-start.14
  146.0 1.5 copy-start.23
  146.1 1.5 copy-start.25
  146.1 1.5 copy-start.29
  146.1 1.5 copy-start.32
  147.6 2.8 copy-start.6
  147.6 2.8 copy-start.19
  147.6 2.8 copy-start.21
  147.6 2.8 copy-start.30
  147.7 2.8 copy-start.31
  224.9 2.2 copy-start.4
  236.2 20.8 %all-to-all-start.2 = ((bf16[32,128,128]{1,2,0:T(8,128)(2,1)}), bf16[32,128,128]{1,2,0:T(8,128)(2,1)S(1)}, u32[]{:S(2)}, u32[]{:S(2)}) async-start(bf16[32,128,128]{1,2,0:T(8,128)(2,1)} %pad_maximum_fusion.1), calls=%async_computation.2 | async-start | bytes 2097152 | tf_op jit(solution)/shard_map/all_to_all | solution.py:37
  257.9 18.6 %all-to-all-start.4 = ((bf16[8,128,64]{1,2,0:T(8,128)(2,1)}), bf16[8,128,64]{1,2,0:T(8,128)(2,1)S(1)}, u32[]{:S(2)}, u32[]{:S(2)}) async-start(bf16[8,128,64]{1,2,0:T(8,128)(2,1)} %broadcast_in_dim.157), calls=%async_computation.4 | async-start | bytes 262144 | tf_op jit(solution)/shard_map/all_to_all | solution.py:43
  277.1 12.9 %all-to-all-start.3 = ((bf16[8,128,64]{1,2,0:T(8,128)(2,1)}), bf16[8,128,64]{1,2,0:T(8,128)(2,1)S(1)}, u32[]{:S(2)}, u32[]{:S(2)}) async-start(bf16[8,128,64]{1,2,0:T(8,128)(2,1)} %broadcast_in_dim.156), calls=%async_computation.3 | async-start | bytes 262144 | tf_op jit(solution)/shard_map/all_to_all | solution.py:43
where the time goes:
time: 295 us; the launch traced here: 291 us
  waiting for transfers between devices  63.4 us (21%)
  matrix products  59.3 us (20%)
  blocking collectives  57.1 us (19%)
  other arithmetic  44.1 us (15%)
  local copies, waits for them, and re-layouts  38.7 us (13%)
  starting transfers between devices  26.4 us (9%)
    all_to_all x1, blocking collectives, sent_together(): lax.all_to_all(both, axis, split_axis=split_dim, concat_axis=concat_dim,...  57.1 us
    dot_general x34, matrix products, contract_axes(): lax.dot_general(first_operand, second_operand, (((first_axis,), (second_a...  53.3 us
    all_to_all x1, waiting for transfers between devices, sent_together(): lax.all_to_all(both, axis, split_axis=split_dim, concat_axis=concat_dim,...  37.4 us
    concatenate x2, local copies, waits for them, and re-layouts, sent_together(): both = jnp.concatenate(arrays, axis=along)  15.7 us
    all_to_all x2, waiting for transfers between devices, copy_for_each(): lax.all_to_all(jnp.broadcast_to(x[None], (length, *x.shape)), axis, 0, 0,...  15.3 us
    all_to_all x2, starting transfers between devices, copy_for_each(): lax.all_to_all(jnp.broadcast_to(x[None], (length, *x.shape)), axis, 0, 0,...  11.8 us
    all_to_all x1, waiting for transfers between devices, sent_and_summed(): tiles = lax.all_to_all(in_blocks(x, dim, length), axis, 0, 0, tiled=True)  10.8 us
    convert_element_type x6, other arithmetic, block_terms(): (probability * (grad_prob - row_delta) * score_scale).astype(jnp.bfloat16)  10.7 us
  transfers between devices with their start and end apart: 4, of which 4 were waited for; matrix products, arithmetic and copies ran while one was open for 7% of the time, Pallas kernels for 0%

commit v1 on v0

v1 whole, which is shorter than its diff:
```python
import functools
import math

import jax
import jax.numpy as jnp
from jax import lax
from jax.experimental import pallas as pl
from jax.experimental.pallas import tpu as pltpu
from jax.sharding import PartitionSpec as P

HEAD = 128
BQ = 256
PAIR = 2 * HEAD
NT = (((1,), (1,)), ((), ()))
NN = (((1,), (0,)), ((), ()))
VM = pl.BlockSpec(memory_space=pltpu.VMEM)
SM = pl.BlockSpec(memory_space=pltpu.SMEM)
rotary_base = 500000.0


def rotary_tables(positions):
    half = HEAD // 2
    frequency = rotary_base ** (-(jnp.arange(half, dtype=jnp.float32) * 2.0 / HEAD))
    angles = positions.astype(jnp.float32)[:, None] * frequency[None, :]
    cos, sin = jnp.cos(angles), jnp.sin(angles)
    return jnp.concatenate([cos, cos], axis=1), jnp.concatenate([-sin, sin], axis=1)


def dot(a, b, dims):
    return lax.dot_general(a, b, dims, preferred_element_type=jnp.float32)


def turn(u, cos, sin):
    return u * cos + pltpu.roll(u, HEAD // 2, 1) * sin


def prep_kernel(place_ref, q_ref, k_ref, v_ref, g_ref, cos_ref, sin_ref, out_ref):
    tok = q_ref.shape[1]
    rollout = pl.program_id(0)
    cos, sin = cos_ref[...], sin_ref[...]
    at = place_ref[0] + lax.broadcasted_iota(jnp.int32, (tok, HEAD), 0)
    keep = (at >= place_ref[1 + rollout]) & (at < place_ref[3 + rollout])

    def turned(ref, lo):
        u = ref[0, :, lo : lo + HEAD].astype(jnp.float32)
        return turn(u, cos, sin).astype(jnp.bfloat16)

    for kv in range(k_ref.shape[2] // HEAD):
        key = turned(k_ref, kv * HEAD)
        value = v_ref[0, :, kv * HEAD : (kv + 1) * HEAD]
        for half in range(2):
            p = 2 * kv + half
            for j in range(2):
                lo = (2 * p + j) * HEAD
                out_ref[p, j * tok : (j + 1) * tok, :] = turned(q_ref, lo)
                g = g_ref[0, :, lo : lo + HEAD]
                out_ref[p, (2 + j) * tok : (3 + j) * tok, :] = jnp.where(keep, g, jnp.zeros_like(g))
            out_ref[p, 4 * tok : 5 * tok, :] = key
            out_ref[p, 5 * tok : 6 * tok, :] = value


def prepare(place, q, k, v, g, cos, sin):
    rollouts, tok, width = q.shape
    parts = 4
    pairs = width // PAIR

    def rows(a):
        return pl.BlockSpec((1, tok, a.shape[2] // parts), lambda r, i: (r, 0, i))

    table = pl.BlockSpec((tok, HEAD), lambda r, i: (0, 0))
    return pl.pallas_call(
        prep_kernel,
        grid=(rollouts, parts),
        out_shape=jax.ShapeDtypeStruct((rollouts * pairs, 6 * tok, HEAD), jnp.bfloat16),
        in_specs=[SM, rows(q), rows(k), rows(v), rows(g), table, table],
        out_specs=pl.BlockSpec((pairs // parts, 6 * tok, HEAD), lambda r, i: (r * parts + i, 0, 0)),
        name="prepare",
    )(place, q, k, v, g, cos, sin)

def attn_kernel(off_ref, x_ref, cos_ref, sin_ref, dq_ref, dkv_ref, s_ref, dp_ref, p_ref, ds_ref, dk_ref, dv_ref, k_ref, kt_ref, v_ref):
    length = dk_ref.shape[0]
    tok = x_ref.shape[1] // 6
    per = BQ // tok
    scale = HEAD ** -0.5
    c = scale * math.log2(math.e)
    off = off_ref[0]
    k_ref[...] = x_ref[:, 4 * tok : 5 * tok, :].reshape(length, HEAD)
    v_ref[...] = x_ref[:, 5 * tok : 6 * tok, :].reshape(length, HEAD)
    kt_ref[...] = k_ref[...].T
    dk_ref[...] = jnp.zeros_like(dk_ref)
    dv_ref[...] = jnp.zeros_like(dv_ref)
    for h in range(2):
        for qb in range(length // BQ):
            end = BQ * (qb + 1)
            q = x_ref[per * qb : per * (qb + 1), tok * h : tok * (h + 1), :].reshape(BQ, HEAD)
            g = x_ref[per * qb : per * (qb + 1), tok * (2 + h) : tok * (3 + h), :].reshape(BQ, HEAD)
            s_ref[:end] = dot(k_ref[:end], q, NT)
            dp_ref[:end] = dot(v_ref[:end], g, NT)
            row = lax.broadcasted_iota(jnp.int32, (BQ, BQ), 0)
            col = lax.broadcasted_iota(jnp.int32, (BQ, BQ), 1)
            last = slice(end - BQ, end)
            if qb == 0:
                seen = (row == col) | ((row >= off) & (row <= col))
                s_ref[last] = jnp.where(seen, s_ref[last], -1e30)
            else:
                s_ref[last] = jnp.where(row <= col, s_ref[last], -1e30)
                first = lax.broadcasted_iota(jnp.int32, (tok, BQ), 0)
                s_ref[:tok] = jnp.where(first >= off, s_ref[:tok], -1e30)
            top = None
            for kb in range(qb + 1):
                t = jnp.max(s_ref[BQ * kb : BQ * (kb + 1)].reshape(BQ // 8, 8, BQ), axis=0)
                top = t if top is None else jnp.maximum(top, t)
            top = jnp.max(top, axis=0, keepdims=True)
            total = jnp.zeros((8, BQ), jnp.float32)
            delta = jnp.zeros((8, BQ), jnp.float32)
            for kb in range(qb + 1):
                rows = slice(BQ * kb, BQ * (kb + 1))
                e = jnp.exp2((s_ref[rows] - top) * c)
                s_ref[rows] = e
                total += jnp.sum(e.reshape(BQ // 8, 8, BQ), axis=0)
                delta += jnp.sum((e * dp_ref[rows]).reshape(BQ // 8, 8, BQ), axis=0)
            inv = 1.0 / jnp.sum(total, axis=0, keepdims=True)
            delta = jnp.sum(delta, axis=0, keepdims=True) * inv
            for kb in range(qb + 1):
                rows = slice(BQ * kb, BQ * (kb + 1))
                p = s_ref[rows] * inv
                p_ref[rows] = p.astype(jnp.bfloat16)
                ds_ref[rows] = (p * ((dp_ref[rows] - delta) * scale)).astype(jnp.bfloat16)
            dv_ref[:end] += dot(p_ref[:end], g, NN)
            dk_ref[:end] += dot(ds_ref[:end], q, NN)
            dq = dot(kt_ref[:, :end], ds_ref[:end], NN).T
            mine = slice(BQ * qb, BQ * (qb + 1))
            dq = turn(dq, cos_ref[mine], sin_ref[mine])
            dq_ref[mine, HEAD * h : HEAD * (h + 1)] = dq.astype(jnp.bfloat16)
    dk = dk_ref[...]
    dkv_ref[:, :HEAD] = turn(dk, cos_ref[...], sin_ref[...]).astype(jnp.bfloat16)
    dkv_ref[:, HEAD:] = dv_ref[...].astype(jnp.bfloat16)


def attend(off, x, cos, sin):
    n = x.shape[0]
    length = n * x.shape[1] // 6
    vm = pl.BlockSpec(memory_space=pltpu.VMEM)
    return pl.pallas_call(
        attn_kernel,
        out_shape=(jax.ShapeDtypeStruct((length, 2 * HEAD), jnp.bfloat16),) * 2,
        in_specs=[pl.BlockSpec(memory_space=pltpu.SMEM), vm, vm, vm],
        out_specs=(vm, vm),
        scratch_shapes=[
            pltpu.VMEM((length, BQ), jnp.float32),
            pltpu.VMEM((length, BQ), jnp.float32),
            pltpu.VMEM((length, BQ), jnp.bfloat16),
            pltpu.VMEM((length, BQ), jnp.bfloat16),
            pltpu.VMEM((length, HEAD), jnp.float32),
            pltpu.VMEM((length, HEAD), jnp.float32),
            pltpu.VMEM((length, HEAD), jnp.bfloat16),
            pltpu.VMEM((HEAD, length), jnp.bfloat16),
            pltpu.VMEM((length, HEAD), jnp.bfloat16),
        ],
        compiler_params=pltpu.CompilerParams(vmem_limit_bytes=40 << 20),
        name="attend",
    )(off, x, cos, sin)

def finish_kernel(y_ref, up_ref, lat_ref, hid_ref, gq_ref, terms_ref):
    rollouts, tok, width = gq_ref.shape
    rank = up_ref.shape[0]
    pairs = width // PAIR
    for r in range(rollouts):
        for p in range(pairs):
            gq_ref[r, :, p * PAIR : (p + 1) * PAIR] = y_ref[r * pairs + p]
    flat = gq_ref[...].reshape(rollouts * tok, width)
    back = dot(flat, up_ref[...], NT).astype(jnp.bfloat16)
    hidden = hid_ref[...].reshape(rollouts * tok, width)
    down = dot(back.T, hidden, NN).astype(jnp.bfloat16)
    upper = dot(lat_ref[...].T, flat, NN).astype(jnp.bfloat16)
    for d in range(width // HEAD):
        terms_ref[d, :rank, :] = down[:, d * HEAD : (d + 1) * HEAD]
        terms_ref[d, rank:, :] = upper[:, d * HEAD : (d + 1) * HEAD]


def finish(y, up, latent, hidden):
    rollouts, tok, width = hidden.shape
    rank = up.shape[0]
    return pl.pallas_call(
        finish_kernel,
        out_shape=(
            jax.ShapeDtypeStruct((rollouts, tok, width), jnp.bfloat16),
            jax.ShapeDtypeStruct((width // HEAD, 2 * rank, HEAD), jnp.bfloat16),
        ),
        in_specs=[VM] * 4,
        out_specs=(VM, VM),
        name="finish",
    )(y, up, latent, hidden)


def keys_kernel(z_ref, gk_ref, gv_ref):
    rollouts, _, width = gk_ref.shape
    groups = width // HEAD
    for r in range(rollouts):
        for kv in range(groups):
            at = 2 * (r * groups + kv)
            both = z_ref[at].astype(jnp.float32) + z_ref[at + 1].astype(jnp.float32)
            both = both.astype(jnp.bfloat16)
            gk_ref[r, :, kv * HEAD : (kv + 1) * HEAD] = both[:, :HEAD]
            gv_ref[r, :, kv * HEAD : (kv + 1) * HEAD] = both[:, HEAD:]


def key_sums(z, shape):
    return pl.pallas_call(
        keys_kernel,
        out_shape=(jax.ShapeDtypeStruct(shape, jnp.bfloat16),) * 2,
        in_specs=[VM],
        out_specs=(VM, VM),
        name="key_sums",
    )(z)


def exchange(x, axis):
    return lax.all_to_all(x, axis, 0, 0, tiled=True)


def on_device(q, k, v, g, hidden, down, up, lengths, offsets):
    rollouts, tok, width = q.shape
    members = lax.axis_size("seq")
    length = tok * members
    me = lax.axis_index("seq")
    cos, sin = rotary_tables(me * tok + jnp.arange(tok, dtype=jnp.int32))
    place = jnp.concatenate([(me * tok)[None].astype(jnp.int32), offsets, lengths])
    x = exchange(prepare(place, q, k, v, g, cos, sin), "seq")
    flat_hidden = hidden.reshape(rollouts * tok, width)
    latent = dot(flat_hidden, down, NN).astype(jnp.bfloat16)
    cos_all, sin_all = rotary_tables(jnp.arange(length, dtype=jnp.int32))
    mine = me // (members // rollouts)
    dq, dkv = attend(lax.dynamic_slice(offsets, (mine,), (1,)), x, cos_all, -sin_all)
    y = exchange(dq.reshape(members, tok, PAIR), "seq")
    z = exchange(dkv.reshape(members, tok, PAIR), "seq")
    grad_query, terms = finish(y, up, latent, hidden)
    terms = jnp.sum(exchange(terms, "seq").astype(jnp.float32), axis=0).astype(jnp.bfloat16)
    copies = lax.axis_size("dp")
    total = exchange(jnp.broadcast_to(terms[None], (copies, *terms.shape)), "dp")
    total = jnp.sum(total.astype(jnp.float32), axis=0)
    grad_key, grad_value = key_sums(z, k.shape)
    rank = up.shape[0]
    return grad_query, grad_key, grad_value, total[:rank].T, total[rank:]


def solution(mesh):
    rows = P("dp", "seq", None)
    return jax.shard_map(
        on_device,
        mesh=mesh,
        in_specs=(rows, rows, rows, rows, rows, P(), P(), P("dp"), P("dp")),
        out_specs=(rows, rows, rows, P("seq", None), P(None, "seq")),
        check_vma=False,
    )
```

time: 295 us -> 174 us (0.59)
  matrix products: 59.3 us -> 1.71 us
  other arithmetic: 44.1 us -> 6.71 us
  Pallas kernels: 0 us -> 36.8 us
  blocking collectives: 57.1 us -> 20.8 us
  local copies, waits for them, and re-layouts: 38.7 us -> 4.7 us
  waiting for transfers between devices: 63.4 us -> 69.1 us
  starting transfers between devices: 26.4 us -> 30 us
    dot_general x42 -> x1, matrix products: 59.3 us -> 1.71 us  [dot(): return lax.dot_general(a, b, dims, preferred_element_type=jnp.float32)]
    pallas_call x0 -> x4, Pallas kernels: none -> 36.8 us  [the longest x1 23.9 us: attend(): pl.pallas_call(attn_kernel, out_shape=(jax.ShapeDtypeStruct((length, 2 *...]
    all_to_all x1, blocking collectives: 57.1 us -> 20.8 us  [exchange(): return lax.all_to_all(x, axis, 0, 0, tiled=True)]
    concatenate x3 -> x0, local copies, waits for them, and re-layouts: 16.6 us -> none  [the longest x2 15.7 us: sent_together(): both = jnp.concatenate(arrays, axis=along)]
    convert_element_type x7 -> x2, other arithmetic: 11.1 us -> 0.01 us  [rotary_tables(): angles = positions.astype(jnp.float32)[:, None] * frequency[None, :]]
    reduce_sum x8 -> x2, other arithmetic: 8.08 us -> 0.19 us  [the longest x1 0.16 us: on_device(): jnp.sum(exchange(terms, 'seq').astype(jnp.float32), axis=0)]
    ge x5 -> x0, other arithmetic: 7.15 us -> none  [block_terms(): col_index >= offset]
    another operation x2 -> x0, other arithmetic: 6.99 us -> none
  transfers between devices with their start and end apart: 4 -> 4, of which waited for: 4 -> 4; matrix products, arithmetic and copies ran while one was open for 7% -> 4% of each run, Pallas kernels for 0% -> 1%
where the time goes in v1:
time: 174 us; the launch traced here: 171 us
  waiting for transfers between devices  69.1 us (40%)
  Pallas kernels  36.8 us (21%)
  starting transfers between devices  30 us (17%)
  blocking collectives  20.8 us (12%)
  other arithmetic  6.71 us (4%)
  local copies, waits for them, and re-layouts  4.7 us (3%)
    all_to_all x4, waiting for transfers between devices, exchange(): return lax.all_to_all(x, axis, 0, 0, tiled=True)  69.1 us
    all_to_all x4, starting transfers between devices, exchange(): return lax.all_to_all(x, axis, 0, 0, tiled=True)  30 us
    pallas_call x1, Pallas kernels, attend(): pl.pallas_call(attn_kernel, out_shape=(jax.ShapeDtypeStruct((length, 2 *...  23.9 us
    all_to_all x1, blocking collectives, exchange(): return lax.all_to_all(x, axis, 0, 0, tiled=True)  20.8 us
    pallas_call x1, Pallas kernels, prepare(): pl.pallas_call(prep_kernel, grid=(rollouts, parts), out_shape=jax.ShapeDt...  6.6 us
    pallas_call x1, Pallas kernels, finish(): pl.pallas_call(finish_kernel, out_shape=(jax.ShapeDtypeStruct((rollouts,...  4.09 us
    neg x2, other arithmetic, rotary_tables(): -sin  3.91 us
  transfers between devices with their start and end apart: 4, of which 4 were waited for; matrix products, arithmetic and copies ran while one was open for 4% of the time, Pallas kernels for 1%

profile of v1, /device:TPU:2, one launch (start us, length us, event | category | flops | bytes accessed | tf_op | source)
XLA Modules:
  0.0 170.7 jit_solution(5811537276608145381)
XLA Ops:
  0.6 0.0 copy-start
  0.7 0.2 fusion.1
  0.9 0.7 pad_maximum_fusion.1
  1.6 1.3 pad_add_fusion.place_ref
  2.9 6.6 %prepare.1 = bf16[32,384,128]{2,1,0:T(8,128)(2,1)} custom-call(s32[5]{0:T(128)} %pad_add_fusion.place_ref, bf16[2,64,4096]{2,1,0:T(8,128)(2,1)} %q_ref.1, bf16[2,64,1024]{2,1,0:T(8,128)(2,1)} %k_ref.1, bf16[2,64,1024]{2,1,0:T(8,128)(2,1)} %v_ref.1, bf16[2,64,4096]{2,1,0:T(8,128)(2,1)} %g_ref.1, f32[64,128]{1,0:T(8,128)} %get-tuple-element.25.cos_ref, ...), custom_call_target="tpu_custom_call" | custom-call | tf_op jit(solution)/shard_map/prepare/pallas_call | solution.py:71
  9.5 0.0 copy-start.4
  9.5 7.8 %all-to-all-start = ((bf16[32,384,128]{2,1,0:T(8,128)(2,1)}), bf16[32,384,128]{2,1,0:T(8,128)(2,1)}, u32[]{:S(2)}, u32[]{:S(2)}) async-start(bf16[32,384,128]{2,1,0:T(8,128)(2,1)} %prepare.1), calls=%async_computation | async-start | bytes 6291456 | tf_op jit(solution)/shard_map/all_to_all | solution.py:219
  17.3 0.0 copy-done.4
  17.3 0.6 dynamic_slice.3.off_ref
  17.9 3.7 %fusion = (f32[2048,64]{1,0:T(8,128)S(1)}, f32[2048,64]{1,0:T(8,128)S(1)}, f32[2048,64]{1,0:T(8,128)S(1)}) fusion(f32[64]{0:T(128)S(1)} %negate_power_fusion, f32[2048]{0:T(1024)S(1)} %iota_convert_fusion), kind=kLoop, calls=%fused_computation.6 | loop fusion | flops 262144 | bytes 1581312 | tf_op jit(solution)/shard_map/neg | solution.py:26
  21.6 0.6 pad_maximum_fusion
  22.2 32.2 %all-to-all-done.x_ref = bf16[32,384,128]{2,1,0:T(8,128)(2,1)} async-done(((bf16[32,384,128]{2,1,0:T(8,128)(2,1)}), bf16[32,384,128]{2,1,0:T(8,128)(2,1)}, u32[]{:S(2)}, u32[]{:S(2)}) %all-to-all-start) | async-done | bytes 3145760 | tf_op jit(solution)/shard_map/all_to_all | solution.py:219
  54.4 23.9 %attend.1 = (bf16[2048,256]{1,0:T(8,128)(2,1)S(1)}, bf16[2048,256]{1,0:T(8,128)(2,1)}) custom-call(s32[1]{0:T(128)} %dynamic_slice.3.off_ref, bf16[32,384,128]{2,1,0:T(8,128)(2,1)} %all-to-all-done.x_ref, f32[2048,128]{1,0:T(8,128)S(1)} %get-tuple-element.27.cos_ref, f32[2048,128]{1,0:T(8,128)S(1)} %get-tuple-element.28.sin_ref), custom_call_target="tpu_custom_call" | custom-call | tf_op jit(solution)/shard_map/attend/pallas_call | solution.py:144
  78.3 0.0 copy-start.1
  78.3 1.0 copy-done.1
  79.3 7.3 %all-to-all-start.1 = ((bf16[32,64,256]{2,1,0:T(8,128)(2,1)}), bf16[32,64,256]{2,1,0:T(8,128)(2,1)S(1)}, u32[]{:S(2)}, u32[]{:S(2)}) async-start(bf16[32,64,256]{2,1,0:T(8,128)(2,1)} %bitcast.8), calls=%async_computation.1 | async-start | bytes 2097152 | tf_op jit(solution)/shard_map/all_to_all | solution.py:219
  86.6 0.0 copy-done
  86.6 1.7 convolution_convert_fusion
  88.4 0.7 copy.16.lat_ref
  89.1 12.0 %all-to-all-done.1.y_ref = bf16[32,64,256]{2,1,0:T(8,128)(2,1)S(1)} async-done(((bf16[32,64,256]{2,1,0:T(8,128)(2,1)}), bf16[32,64,256]{2,1,0:T(8,128)(2,1)S(1)}, u32[]{:S(2)}, u32[]{:S(2)}) %all-to-all-start.1) | async-done | bytes 1048608 | tf_op jit(solution)/shard_map/all_to_all | solution.py:219
  101.0 0.0 copy-start.3
  101.0 1.0 copy-done.3
  102.0 4.1 %finish.1 = (bf16[2,64,4096]{2,1,0:T(8,128)(2,1)}, bf16[32,128,128]{2,1,0:T(8,128)(2,1)}) custom-call(bf16[32,64,256]{2,1,0:T(8,128)(2,1)} %copy-done.3, bf16[64,4096]{1,0:T(8,128)(2,1)} %up_ref.1, bf16[128,64]{1,0:T(8,128)(2,1)} %copy.16.lat_ref, bf16[2,64,4096]{2,1,0:T(8,128)(2,1)} %hid_ref.1), custom_call_target="tpu_custom_call" | custom-call | tf_op jit(solution)/shard_map/finish/pallas_call | solution.py:184
  106.1 20.8 %all_to_all.25 = bf16[32,128,128]{2,1,0:T(8,128)(2,1)S(1)} all-to-all(bf16[32,128,128]{2,1,0:T(8,128)(2,1)} %get-tuple-element.16), channel_id=1, replica_groups=mesh['seq'=32,'dp'=8] {'seq'}, dimensions={0} | all-to-all | bytes 2097152 | tf_op jit(solution)/shard_map/all_to_all | solution.py:219
  126.9 6.4 %all-to-all-start.2 = ((bf16[32,64,256]{2,1,0:T(8,128)(2,1)}), bf16[32,64,256]{2,1,0:T(8,128)(2,1)S(1)}, u32[]{:S(2)}, u32[]{:S(2)}) async-start(bf16[32,64,256]{2,1,0:T(8,128)(2,1)} %bitcast.3), calls=%async_computation.2 | async-start | bytes 2097152 | tf_op jit(solution)/shard_map/all_to_all | solution.py:219
  133.4 0.2 reduce_sum.21
  133.5 14.3 %all-to-all-done.2.z_ref = bf16[32,64,256]{2,1,0:T(8,128)(2,1)S(1)} async-done(((bf16[32,64,256]{2,1,0:T(8,128)(2,1)}), bf16[32,64,256]{2,1,0:T(8,128)(2,1)S(1)}, u32[]{:S(2)}, u32[]{:S(2)}) %all-to-all-start.2) | async-done | bytes 1048608 | tf_op jit(solution)/shard_map/all_to_all | solution.py:219
  147.8 0.0 copy-start.2
  147.8 0.8 broadcast_in_dim.5
  148.6 8.5 %all-to-all-start.4 = ((bf16[8,128,128]{2,1,0:T(8,128)(2,1)}), bf16[8,128,128]{2,1,0:T(8,128)(2,1)S(1)}, u32[]{:S(2)}, u32[]{:S(2)}) async-start(bf16[8,128,128]{2,1,0:T(8,128)(2,1)} %broadcast_in_dim.5), calls=%async_computation.4 | async-start | bytes 524288 | tf_op jit(solution)/shard_map/all_to_all | solution.py:219
  157.0 0.0 copy-done.2
  157.1 2.2 %key_sums.1 = (bf16[2,64,1024]{2,1,0:T(8,128)(2,1)}, bf16[2,64,1024]{2,1,0:T(8,128)(2,1)}) custom-call(bf16[32,64,256]{2,1,0:T(8,128)(2,1)} %copy-done.2), custom_call_target="tpu_custom_call" | custom-call | tf_op jit(solution)/shard_map/key_sums/pallas_call | solution.py:209
  159.2 10.8 %all-to-all-done.4 = bf16[8,128,128]{2,1,0:T(8,128)(2,1)S(1)} async-done(((bf16[8,128,128]{2,1,0:T(8,128)(2,1)}), bf16[8,128,128]{2,1,0:T(8,128)(2,1)S(1)}, u32[]{:S(2)}, u32[]{:S(2)}) %all-to-all-start.4) | async-done | bytes 262176 | tf_op jit(solution)/shard_map/all_to_all | solution.py:219
  170.0 0.6 fusion.2
  (4 shorter events, 0.1 us)
Async XLA Ops:
  0.6 86.0 %copy-start = (bf16[4096,64]{0,1:T(8,128)(2,1)S(1)}, bf16[4096,64]{0,1:T(8,128)(2,1)}, u32[]{:S(2)}) copy-start(bf16[4096,64]{0,1:T(8,128)(2,1)} %param.14) | copy-start | bytes 1572868
  9.5 7.8 %copy-start.4 = (s32[2]{0:T(128)S(1)}, s32[2]{0:T(128)}, u32[]{:S(2)}) copy-start(s32[2]{0:T(128)} %param.17) | copy-start | bytes 28
  9.5 44.9 %all-to-all-start = ((bf16[32,384,128]{2,1,0:T(8,128)(2,1)}), bf16[32,384,128]{2,1,0:T(8,128)(2,1)}, u32[]{:S(2)}, u32[]{:S(2)}) async-start(bf16[32,384,128]{2,1,0:T(8,128)(2,1)} %prepare.1), calls=%async_computation | async-start | bytes 6291456 | tf_op jit(solution)/shard_map/all_to_all | solution.py:219
  78.3 1.0 copy-start.1
  79.3 21.7 %all-to-all-start.1 = ((bf16[32,64,256]{2,1,0:T(8,128)(2,1)}), bf16[32,64,256]{2,1,0:T(8,128)(2,1)S(1)}, u32[]{:S(2)}, u32[]{:S(2)}) async-start(bf16[32,64,256]{2,1,0:T(8,128)(2,1)} %bitcast.8), calls=%async_computation.1 | async-start | bytes 2097152 | tf_op jit(solution)/shard_map/all_to_all | solution.py:219
  101.0 1.0 copy-start.3
  126.9 20.8 %all-to-all-start.2 = ((bf16[32,64,256]{2,1,0:T(8,128)(2,1)}), bf16[32,64,256]{2,1,0:T(8,128)(2,1)S(1)}, u32[]{:S(2)}, u32[]{:S(2)}) async-start(bf16[32,64,256]{2,1,0:T(8,128)(2,1)} %bitcast.3), calls=%async_computation.2 | async-start | bytes 2097152 | tf_op jit(solution)/shard_map/all_to_all | solution.py:219
  147.8 9.3 %copy-start.2 = (bf16[32,64,256]{2,1,0:T(8,128)(2,1)}, bf16[32,64,256]{2,1,0:T(8,128)(2,1)S(1)}, u32[]{:S(2)}) copy-start(bf16[32,64,256]{2,1,0:T(8,128)(2,1)S(1)} %all-to-all-done.2.z_ref) | copy-start | bytes 3145732
  148.6 21.4 %all-to-all-start.4 = ((bf16[8,128,128]{2,1,0:T(8,128)(2,1)}), bf16[8,128,128]{2,1,0:T(8,128)(2,1)S(1)}, u32[]{:S(2)}, u32[]{:S(2)}) async-start(bf16[8,128,128]{2,1,0:T(8,128)(2,1)} %broadcast_in_dim.5), calls=%async_computation.4 | async-start | bytes 524288 | tf_op jit(solution)/shard_map/all_to_all | solution.py:219

commit v2 on v1

v2 whole, which is shorter than its diff:
```python
import math

import jax
import jax.numpy as jnp
import numpy as np
from jax import lax
from jax.experimental import pallas as pl
from jax.experimental.pallas import tpu as pltpu
from jax.sharding import PartitionSpec as P


HEAD = 128
BQ = 256
PAIR = 2 * HEAD
NT = (((1,), (1,)), ((), ()))
NN = (((1,), (0,)), ((), ()))
VM = pl.BlockSpec(memory_space=pltpu.VMEM)
SM = pl.BlockSpec(memory_space=pltpu.SMEM)
rotary_base = 500000.0


def rotary_tables(positions):
    half = HEAD // 2
    frequency = (rotary_base ** (-(np.arange(half) * 2.0 / HEAD))).astype(np.float32)
    angles = positions.astype(jnp.float32)[:, None] * frequency[None, :]
    return jnp.concatenate([jnp.cos(angles), jnp.sin(angles)], axis=1)


def spread(table, sign):
    other = pltpu.roll(table, HEAD // 2, 1)
    low = lax.broadcasted_iota(jnp.int32, table.shape, 1) < HEAD // 2
    return jnp.where(low, table, other), jnp.where(low, -sign * other, sign * table)


def dot(a, b, dims):
    return lax.dot_general(a, b, dims, preferred_element_type=jnp.float32)


def turn(u, cos, sin):
    return u * cos + pltpu.roll(u, HEAD // 2, 1) * sin


def in_hbm(*arrays):
    return [pltpu.with_memory_space_constraint(a, pltpu.HBM) for a in arrays]


def in_vmem(*arrays):
    return [pltpu.with_memory_space_constraint(a, pltpu.VMEM) for a in arrays]


def prep_kernel(off_ref, len_ref, q_ref, k_ref, v_ref, g_ref, table_ref, out_ref):
    tok = q_ref.shape[1]
    part = tok // 2
    rollout = pl.program_id(0)
    cos, sin = spread(table_ref[...], 1.0)
    at = lax.axis_index("seq") * tok + lax.broadcasted_iota(jnp.int32, (tok, HEAD), 0)
    keep = (at >= off_ref[rollout]) & (at < len_ref[rollout])

    def turned(ref, lo):
        u = ref[0, :, lo : lo + HEAD].astype(jnp.float32)
        return turn(u, cos, sin).astype(jnp.bfloat16)

    for kv in range(k_ref.shape[2] // HEAD):
        key = turned(k_ref, kv * HEAD)
        value = v_ref[0, :, kv * HEAD : (kv + 1) * HEAD]
        for half in range(2):
            p = 2 * kv + half
            for j in range(2):
                lo = (2 * p + j) * HEAD
                out_ref[p, j * tok : (j + 1) * tok, :] = turned(q_ref, lo)
                g = g_ref[0, :, lo : lo + HEAD]
                out_ref[p, (2 + j) * tok : (3 + j) * tok, :] = jnp.where(keep, g, jnp.zeros_like(g))
            mine = slice(half * part, (half + 1) * part)
            out_ref[p, 4 * tok : 4 * tok + part, :] = key[mine]
            out_ref[p, 4 * tok + part :, :] = value[mine]


def prepare(offsets, lengths, q, k, v, g, table):
    rollouts, tok, width = q.shape
    parts = 1
    pairs = width // PAIR

    def rows(a):
        return pl.BlockSpec((1, tok, a.shape[2] // parts), lambda r, i: (r, 0, i))

    whole = pl.BlockSpec((tok, HEAD), lambda r, i: (0, 0))
    return pl.pallas_call(
        prep_kernel,
        grid=(rollouts, parts),
        out_shape=pltpu.HBM((rollouts * pairs, 5 * tok, HEAD), jnp.bfloat16),
        in_specs=[SM, SM, rows(q), rows(k), rows(v), rows(g), whole],
        out_specs=pl.BlockSpec((pairs // parts, 5 * tok, HEAD), lambda r, i: (r * parts + i, 0, 0)),
        compiler_params=pltpu.CompilerParams(vmem_limit_bytes=16 << 20),
        name="prepare",
    )(*in_hbm(offsets, lengths, q, k, v, g), table)


def attn_kernel(
    off_ref,
    x_ref,
    other_ref,
    table_hbm,
    dq_hbm,
    keep_hbm,
    give_hbm,
    table_ref,
    dq_ref,
    s_ref,
    dp_ref,
    p_ref,
    ds_ref,
    dk_ref,
    dv_ref,
    k4_ref,
    v4_ref,
    kt_ref,
    k_ref,
    v_ref,
    sum_ref,
    sems,
):
    length = dk_ref.shape[0]
    tok = x_ref.shape[1] // 5
    part = tok // 2
    place = lax.axis_index("seq")
    half = place % 2
    off = off_ref[place // (x_ref.shape[0] // off_ref.shape[0])]
    per = BQ // tok
    blocks = length // BQ
    scale = HEAD ** -0.5
    c = scale * math.log2(math.e)
    fetch = pltpu.make_async_copy(table_hbm, table_ref, sems.at[0])
    fetch.start()
    k4_ref[:, half] = x_ref[:, 4 * tok : 4 * tok + part, :]
    v4_ref[:, half] = x_ref[:, 4 * tok + part :, :]
    k4_ref[:, 1 - half] = other_ref[:, :part, :]
    v4_ref[:, 1 - half] = other_ref[:, part:, :]
    k_ref[...] = k4_ref[...].reshape(length, HEAD)
    v_ref[...] = v4_ref[...].reshape(length, HEAD)
    kt_ref[...] = k_ref[...].T
    dk_ref[...] = jnp.zeros_like(dk_ref)
    dv_ref[...] = jnp.zeros_like(dv_ref)
    units = [(h, qb) for qb in range(blocks) for h in range(2)]

    def operands(u):
        h, qb = units[u]
        at = slice(per * qb, per * (qb + 1))
        q = x_ref[at, tok * h : tok * (h + 1), :].reshape(BQ, HEAD)
        g = x_ref[at, tok * (2 + h) : tok * (3 + h), :].reshape(BQ, HEAD)
        return u % 2, BQ * (units[u][1] + 1), q, g

    def scores(u):
        b, end, q, g = operands(u)
        s_ref[b, :end] = dot(k_ref[:end], q, NT)
        dp_ref[b, :end] = dot(v_ref[:end], g, NT)

    def weigh(u):
        b, end, _, _ = operands(u)
        qb = units[u][1]
        row = lax.broadcasted_iota(jnp.int32, (BQ, BQ), 0)
        col = lax.broadcasted_iota(jnp.int32, (BQ, BQ), 1)
        last = slice(end - BQ, end)
        if qb == 0:
            seen = (row == col) | ((row >= off) & (row <= col))
            s_ref[b, last] = jnp.where(seen, s_ref[b, last], -1e30)
        else:
            s_ref[b, last] = jnp.where(row <= col, s_ref[b, last], -1e30)
            early = lax.broadcasted_iota(jnp.int32, (tok, BQ), 0)
            s_ref[b, :tok] = jnp.where(early >= off, s_ref[b, :tok], -1e30)
        top = None
        for kb in range(qb + 1):
            t = jnp.max(s_ref[b, BQ * kb : BQ * (kb + 1)].reshape(BQ // 8, 8, BQ), axis=0)
            top = t if top is None else jnp.maximum(top, t)
        top = jnp.max(top, axis=0, keepdims=True)
        total = jnp.zeros((8, BQ), jnp.float32)
        delta = jnp.zeros((8, BQ), jnp.float32)
        for kb in range(qb + 1):
            rows = slice(BQ * kb, BQ * (kb + 1))
            e = jnp.exp2((s_ref[b, rows] - top) * c)
            s_ref[b, rows] = e
            total += jnp.sum(e.reshape(BQ // 8, 8, BQ), axis=0)
            delta += jnp.sum((e * dp_ref[b, rows]).reshape(BQ // 8, 8, BQ), axis=0)
        inv = 1.0 / jnp.sum(total, axis=0, keepdims=True)
        delta = jnp.sum(delta, axis=0, keepdims=True) * inv
        for kb in range(qb + 1):
            rows = slice(BQ * kb, BQ * (kb + 1))
            e = s_ref[b, rows]
            p_ref[b, rows] = (e * inv).astype(jnp.bfloat16)
            ds_ref[b, rows] = (e * (inv * scale) * (dp_ref[b, rows] - delta)).astype(jnp.bfloat16)

    def rows_out(qb):
        mine = slice(BQ * qb, BQ * (qb + 1))
        return pltpu.make_async_copy(dq_ref.at[mine], dq_hbm.at[mine], sems.at[3 + qb])

    def spend(u):
        b, end, q, g = operands(u)
        h, qb = units[u]
        dv_ref[:end] += dot(p_ref[b, :end], g, NN)
        dk_ref[:end] += dot(ds_ref[b, :end], q, NN)
        dq = dot(kt_ref[:, :end], ds_ref[b, :end], NN).T
        mine = slice(BQ * qb, BQ * (qb + 1))
        dq = turn(dq, *spread(table_ref[mine], -1.0))
        dq_ref[mine, HEAD * h : HEAD * (h + 1)] = dq.astype(jnp.bfloat16)
        if h == 1:
            rows_out(qb).start()

    scores(0)
    fetch.wait()
    for u in range(len(units)):
        if u + 1 < len(units):
            scores(u + 1)
        weigh(u)
        spend(u)
    shape = k4_ref.shape
    sum_ref[:, :, :, :HEAD] = turn(dk_ref[...], *spread(table_ref[...], -1.0)).astype(jnp.bfloat16).reshape(shape)
    sum_ref[:, :, :, HEAD:] = dv_ref[...].astype(jnp.bfloat16).reshape(shape)
    give = pltpu.make_async_copy(sum_ref.at[:, 1 - half], give_hbm, sems.at[1])
    give.start()
    keep = pltpu.make_async_copy(sum_ref.at[:, half], keep_hbm, sems.at[2])
    keep.start()
    for qb in range(blocks):
        rows_out(qb).wait()
    give.wait()
    keep.wait()


def attend(offsets, x, other, table):
    n = x.shape[0]
    length = n * x.shape[1] // 5
    part = length // n // 2
    halves = (n, 2, part, HEAD)
    hbm = pl.BlockSpec(memory_space=pltpu.HBM)
    f32, low = jnp.float32, jnp.bfloat16
    return pl.pallas_call(
        attn_kernel,
        out_shape=(
            pltpu.HBM((length, PAIR), low),
            pltpu.HBM((n, part, PAIR), low),
            pltpu.HBM((n, part, PAIR), low),
        ),
        in_specs=[SM, VM, VM, hbm],
        out_specs=(hbm, hbm, hbm),
        scratch_shapes=[
            pltpu.VMEM((length, HEAD), f32),
            pltpu.VMEM((length, PAIR), low),
            pltpu.VMEM((2, length, BQ), f32),
            pltpu.VMEM((2, length, BQ), f32),
            pltpu.VMEM((2, length, BQ), low),
            pltpu.VMEM((2, length, BQ), low),
            pltpu.VMEM((length, HEAD), f32),
            pltpu.VMEM((length, HEAD), f32),
            pltpu.VMEM(halves, low),
            pltpu.VMEM(halves, low),
            pltpu.VMEM((HEAD, length), low),
            pltpu.VMEM((length, HEAD), low),
            pltpu.VMEM((length, HEAD), low),
            pltpu.VMEM((n, 2, part, PAIR), low),
            pltpu.SemaphoreType.DMA((3 + length // BQ,)),
        ],
        compiler_params=pltpu.CompilerParams(vmem_limit_bytes=40 << 20),
        cost_estimate=pl.CostEstimate(flops=24 * 10**9, bytes_accessed=8 << 20, transcendentals=6 * 10**6),
        name="attend",
    )(*in_hbm(offsets), *in_vmem(x, other), *in_hbm(table))


def keys_of_kernel(x_ref, out_ref):
    rows = out_ref.shape[1]
    out_ref[...] = x_ref[:, x_ref.shape[1] - rows :, :]


def keys_of(x):
    n, rows, width = x.shape
    return pl.pallas_call(
        keys_of_kernel,
        out_shape=pltpu.VMEM((n, rows // 5, width), x.dtype),
        in_specs=[VM],
        out_specs=VM,
        compiler_params=pltpu.CompilerParams(vmem_limit_bytes=8 << 20),
        name="keys_of",
    )(*in_vmem(x))


def finish_kernel(y_ref, up_ref, lat_ref, hid_ref, gq_hbm, terms_hbm, gq_ref, terms_ref, sems):
    rollouts, tok, width = gq_ref.shape
    rank = up_ref.shape[0]
    pairs = width // PAIR
    for r in range(rollouts):
        for p in range(pairs):
            gq_ref[r, :, p * PAIR : (p + 1) * PAIR] = y_ref[r * pairs + p]
    save = pltpu.make_async_copy(gq_ref, gq_hbm, sems.at[0])
    save.start()
    flat = gq_ref[...].reshape(rollouts * tok, width)
    back = dot(flat, up_ref[...], NT).astype(jnp.bfloat16).T
    latent = lat_ref[...].T
    hidden = hid_ref[...].reshape(rollouts * tok, width)
    pieces = sems.shape[0] - 1
    each = width // HEAD // pieces
    sends = []
    for i in range(pieces):
        cols = slice(i * each * HEAD, (i + 1) * each * HEAD)
        down = dot(back, hidden[:, cols], NN).astype(jnp.bfloat16)
        upper = dot(latent, flat[:, cols], NN).astype(jnp.bfloat16)
        for d in range(each):
            terms_ref[i * each + d, :rank, :] = down[:, d * HEAD : (d + 1) * HEAD]
            terms_ref[i * each + d, rank:, :] = upper[:, d * HEAD : (d + 1) * HEAD]
        at = slice(i * each, (i + 1) * each)
        sends.append(pltpu.make_async_copy(terms_ref.at[at], terms_hbm.at[at], sems.at[1 + i]))
        sends[-1].start()
    save.wait()
    for send in sends:
        send.wait()


def finish(y, up, latent, hidden):
    rollouts, tok, width = hidden.shape
    rank = up.shape[0]
    terms = (width // HEAD, 2 * rank, HEAD)
    hbm = pl.BlockSpec(memory_space=pltpu.HBM)
    return pl.pallas_call(
        finish_kernel,
        out_shape=(pltpu.HBM((rollouts, tok, width), jnp.bfloat16), pltpu.HBM(terms, jnp.bfloat16)),
        in_specs=[VM] * 4,
        out_specs=(hbm, hbm),
        scratch_shapes=[
            pltpu.VMEM((rollouts, tok, width), jnp.bfloat16),
            pltpu.VMEM(terms, jnp.bfloat16),
            pltpu.SemaphoreType.DMA((5,)),
        ],
        compiler_params=pltpu.CompilerParams(vmem_limit_bytes=16 << 20),
        name="finish",
    )(*in_vmem(y, up, latent, hidden))


def keys_kernel(z_ref, gk_ref, gv_ref):
    rollouts, tok, width = gk_ref.shape
    groups = width // HEAD
    part = tok // 2
    for r in range(rollouts):
        for kv in range(groups):
            for half in range(2):
                both = z_ref[2 * (r * groups + kv) + half]
                rows = slice(half * part, (half + 1) * part)
                gk_ref[r, rows, kv * HEAD : (kv + 1) * HEAD] = both[:, :HEAD]
                gv_ref[r, rows, kv * HEAD : (kv + 1) * HEAD] = both[:, HEAD:]


def key_sums(z, shape):
    return pl.pallas_call(
        keys_kernel,
        out_shape=(jax.ShapeDtypeStruct(shape, jnp.bfloat16),) * 2,
        in_specs=[VM],
        out_specs=(VM, VM),
        compiler_params=pltpu.CompilerParams(vmem_limit_bytes=8 << 20),
        name="key_sums",
    )(*in_vmem(z))


def exchange(x, axis):
    return lax.all_to_all(x, axis, 0, 0, tiled=True)


def swap(x, axis, bit):
    return lax.ppermute(x, axis, [(i, i ^ bit) for i in range(lax.axis_size(axis))])


def on_device(q, k, v, g, hidden, down, up, lengths, offsets):
    rollouts, tok, width = q.shape
    members = lax.axis_size("seq")
    length = tok * members
    own = rotary_tables(lax.axis_index("seq") * tok + jnp.arange(tok, dtype=jnp.int32))
    x = prepare(offsets, lengths, q, k, v, g, own)
    x = exchange(x, "seq")
    other = swap(keys_of(x), "seq", 1)
    flat_hidden = hidden.reshape(rollouts * tok, width)
    latent = dot(flat_hidden, down, NN).astype(jnp.bfloat16)
    table = rotary_tables(jnp.arange(length, dtype=jnp.int32))
    dq, keep, give = attend(offsets, x, other, table)
    y = exchange(dq.reshape(members, tok, PAIR), "seq")
    both = (keep.astype(jnp.float32) + swap(give, "seq", 1).astype(jnp.float32)).astype(jnp.bfloat16)
    grad_query, terms = finish(y, up, latent, hidden)
    terms = exchange(terms, "seq")
    both, terms = lax.optimization_barrier((both, terms))
    z = exchange(both, "seq")
    total = jnp.sum(terms.astype(jnp.float32), axis=0)
    bit = 1
    while bit < lax.axis_size("dp"):
        low = total.astype(jnp.bfloat16)
        got = swap(low, "dp", bit)
        total = low.astype(jnp.float32) + got.astype(jnp.float32)
        bit *= 2
    grad_key, grad_value = key_sums(z, k.shape)
    rank = up.shape[0]
    return grad_query, grad_key, grad_value, total[:rank].T, total[rank:]


def solution(mesh):
    rows = P("dp", "seq", None)

    return jax.shard_map(
        on_device,
        mesh=mesh,
        in_specs=(rows, rows, rows, rows, rows, P(), P(), P("dp"), P("dp")),
        out_specs=(rows, rows, rows, P("seq", None), P(None, "seq")),
        check_vma=False,
    )
```

time: 174 us -> 142 us (0.82)
  the two profiles are of different devices: /device:TPU:2 before, /device:TPU:1 now
where the time goes in v2:
time: 142 us
  waiting for transfers between devices  70.3 us (50%)
  starting transfers between devices  33 us (23%)
  Pallas kernels  26.8 us (19%)
  other arithmetic  8.22 us (6%)
  matrix products  1.7 us (1%)
    all_to_all x4, waiting for transfers between devices, exchange(): return lax.all_to_all(x, axis, 0, 0, tiled=True)  65.5 us
    all_to_all x4, starting transfers between devices, exchange(): return lax.all_to_all(x, axis, 0, 0, tiled=True)  21.5 us
    pallas_call x1, Pallas kernels, attend(): pl.pallas_call(attn_kernel, out_shape=(pltpu.HBM((length, PAIR), low), pl...  20.4 us
    ppermute x5, starting transfers between devices, swap(): lax.ppermute(x, axis, [(i, i ^ bit) for i in range(lax.axis_size(axis))])  11.5 us
    ppermute x5, waiting for transfers between devices, swap(): lax.ppermute(x, axis, [(i, i ^ bit) for i in range(lax.axis_size(axis))])  4.76 us
    cos x2, other arithmetic, rotary_tables(): return jnp.concatenate([jnp.cos(angles), jnp.sin(angles)], axis=1)  4.59 us
    pallas_call x1, Pallas kernels, prepare(): pl.pallas_call(prep_kernel, grid=(rollouts, parts), out_shape=pltpu.HBM((...  3.35 us
  transfers between devices with their start and end apart: 9, of which 7 were waited for; matrix products, arithmetic and copies ran while one was open for 7% of the time, Pallas kernels for 0%

profile of v2, /device:TPU:1, one launch (start us, length us, event | category | flops | bytes accessed | tf_op | source)
XLA Modules:
  0.0 141.6 jit_solution(4203587179816153935)
XLA Ops:
  0.6 0.0 copy-start
  0.7 0.9 multiply_cosine_fusion.1
  1.6 0.1 pad_maximum_fusion.1.table_ref
  1.6 3.4 %prepare.1 = bf16[32,320,128]{2,1,0:T(8,128)(2,1)} custom-call(s32[2]{0:T(128)} %off_ref.3, s32[2]{0:T(128)} %len_ref.1, bf16[2,64,4096]{2,1,0:T(8,128)(2,1)} %q_ref.1, bf16[2,64,1024]{2,1,0:T(8,128)(2,1)} %k_ref.1, bf16[2,64,1024]{2,1,0:T(8,128)(2,1)} %v_ref.1, bf16[2,64,4096]{2,1,0:T(8,128)(2,1)} %g_ref.1, f32[64,128]{1,0:T(8,128)S(1)} %pad_maximum_fusion.1.table_ref), custom_call_target="tpu_custom_call" | custom-call | tf_op jit(solution)/shard_map/prepare/pallas_call | solution.py:87
  5.0 8.6 %all-to-all-start = ((bf16[32,320,128]{2,1,0:T(8,128)(2,1)}), bf16[32,320,128]{2,1,0:T(8,128)(2,1)S(1)}, u32[]{:S(2)}, u32[]{:S(2)}) async-start(bf16[32,320,128]{2,1,0:T(8,128)(2,1)} %prepare.1), calls=%async_computation | async-start | bytes 5242880 | tf_op jit(solution)/shard_map/all_to_all | solution.py:359
  13.6 0.0 copy-start.3
  13.6 33.9 %all-to-all-done.x_ref = bf16[32,320,128]{2,1,0:T(8,128)(2,1)S(1)} async-done(((bf16[32,320,128]{2,1,0:T(8,128)(2,1)}), bf16[32,320,128]{2,1,0:T(8,128)(2,1)S(1)}, u32[]{:S(2)}, u32[]{:S(2)}) %all-to-all-start) | async-done | bytes 2621472 | tf_op jit(solution)/shard_map/all_to_all | solution.py:359
  47.5 1.0 collective-permute-start
  48.5 0.0 copy-done.3
  48.5 3.7 %multiply_cosine_fusion = (f32[2048,64]{1,0:T(8,128)S(1)}, f32[2048,64]{1,0:T(8,128)S(1)}) fusion(f32[64]{0:T(128)S(1)} %copy-done.3, f32[2048]{0:T(1024)S(1)} %iota_convert_fusion), kind=kLoop, calls=%fused_computation.1 | loop fusion | flops 131072 | bytes 1057024 | tf_op jit(solution)/shard_map/cos | solution.py:26
  52.2 1.3 pad_maximum_fusion.table_hbm
  53.5 0.0 collective-permute-done.other_ref
  53.5 20.4 %attend.1 = (bf16[2048,256]{1,0:T(8,128)(2,1)}, bf16[32,32,256]{2,1,0:T(8,128)(2,1)}, bf16[32,32,256]{2,1,0:T(8,128)(2,1)}) custom-call(s32[2]{0:T(128)} %off_ref.3, bf16[32,320,128]{2,1,0:T(8,128)(2,1)S(1)} %all-to-all-done.x_ref, bf16[32,64,128]{2,1,0:T(8,128)(2,1)S(1)} %collective-permute-done.other_ref, f32[2048,128]{1,0:T(8,128)} %pad_maximum_fusion.table_hbm), custom_call_target="tpu_custom_call" | custom-call | flops 24000000000 | bytes 8388608 | tf_op jit(solution)/shard_map/attend/pallas_call | solution.py:234
  73.9 0.0 copy-start.1
  73.9 0.0 copy-start.2
  73.9 3.9 %all-to-all-start.1 = ((bf16[32,64,256]{2,1,0:T(8,128)(2,1)}), bf16[32,64,256]{2,1,0:T(8,128)(2,1)S(1)}, u32[]{:S(2)}, u32[]{:S(2)}) async-start(bf16[32,64,256]{2,1,0:T(8,128)(2,1)} %bitcast.7), calls=%async_computation.1 | async-start | bytes 2097152 | tf_op jit(solution)/shard_map/all_to_all | solution.py:359
  77.8 0.0 copy-done
  77.8 1.7 %convolution_convert_fusion = bf16[128,64]{0,1:T(8,128)(2,1)S(1)} fusion(bf16[128,4096]{1,0:T(8,128)(2,1)} %bitcast.6, bf16[4096,64]{0,1:T(8,128)(2,1)S(1)} %copy-done), kind=kOutput, calls=%fused_computation.2 | convolution fusion | flops 67117056 | bytes 1589248 | tf_op jit(solution)/shard_map/dot_general | solution.py:36
  79.5 0.1 copy.17.lat_ref
  79.6 15.1 %all-to-all-done.1.y_ref = bf16[32,64,256]{2,1,0:T(8,128)(2,1)S(1)} async-done(((bf16[32,64,256]{2,1,0:T(8,128)(2,1)}), bf16[32,64,256]{2,1,0:T(8,128)(2,1)S(1)}, u32[]{:S(2)}, u32[]{:S(2)}) %all-to-all-start.1) | async-done | bytes 1048608 | tf_op jit(solution)/shard_map/all_to_all | solution.py:359
  94.7 0.0 copy-done.1
  94.7 0.0 copy-done.2
  94.7 2.1 %finish.1 = (bf16[2,64,4096]{2,1,0:T(8,128)(2,1)}, bf16[32,128,128]{2,1,0:T(8,128)(2,1)}) custom-call(bf16[32,64,256]{2,1,0:T(8,128)(2,1)S(1)} %all-to-all-done.1.y_ref, bf16[64,4096]{1,0:T(8,128)(2,1)S(1)} %copy-done.2, bf16[128,64]{1,0:T(8,128)(2,1)S(1)} %copy.17.lat_ref, bf16[2,64,4096]{2,1,0:T(8,128)(2,1)S(1)} %copy-done.1), custom_call_target="tpu_custom_call" | custom-call | tf_op jit(solution)/shard_map/finish/pallas_call | solution.py:319
  96.8 3.9 %all-to-all-start.2 = ((bf16[32,128,128]{2,1,0:T(8,128)(2,1)}), bf16[32,128,128]{2,1,0:T(8,128)(2,1)S(1)}, u32[]{:S(2)}, u32[]{:S(2)}) async-start(bf16[32,128,128]{2,1,0:T(8,128)(2,1)} %get-tuple-element.18), calls=%async_computation.2 | async-start | bytes 2097152 | tf_op jit(solution)/shard_map/all_to_all | solution.py:359
  100.8 0.5 collective-permute-start.1
  101.3 1.9 %collective-permute-done.1 = bf16[32,32,256]{2,1,0:T(8,128)(2,1)S(1)} collective-permute-done((bf16[32,32,256]{2,1,0:T(8,128)(2,1)}, bf16[32,32,256]{2,1,0:T(8,128)(2,1)S(1)}, u32[]{:S(2)}, u32[]{:S(2)}) %collective-permute-start.1) | collective-permute-done | bytes 524320 | tf_op jit(solution)/shard_map/ppermute | solution.py:363
  103.2 2.0 %add_convert_fusion = bf16[32,32,256]{2,1,0:T(8,128)(2,1)} fusion(bf16[32,32,256]{2,1,0:T(8,128)(2,1)S(1)} %collective-permute-done.1, bf16[32,32,256]{2,1,0:T(8,128)(2,1)} %get-tuple-element.16), kind=kLoop, calls=%fused_computation.4 | loop fusion | flops 1048576 | bytes 1572864 | tf_op jit(solution)/shard_map/convert_element_type | solution.py:379
  105.2 12.4 %all-to-all-done.2 = bf16[32,128,128]{2,1,0:T(8,128)(2,1)S(1)} async-done(((bf16[32,128,128]{2,1,0:T(8,128)(2,1)}), bf16[32,128,128]{2,1,0:T(8,128)(2,1)S(1)}, u32[]{:S(2)}, u32[]{:S(2)}) %all-to-all-start.2) | async-done | bytes 1048608 | tf_op jit(solution)/shard_map/all_to_all | solution.py:359
  117.7 0.2 reduce_sum.12
  117.8 1.7 %collective-permute-start.2 = (bf16[128,128]{1,0:T(8,128)(2,1)S(1)}, bf16[128,128]{1,0:T(8,128)(2,1)S(1)}, u32[]{:S(2)}, u32[]{:S(2)}) collective-permute-start(bf16[128,128]{1,0:T(8,128)(2,1)S(1)} %reduce_sum.12), channel_id=1, source_target_pairs={{0,1},{1,0},{2,3},{3,2},{4,5},{5,4},{6,7},{7,6},{8,9},{9,8},{10,11... | collective-permute-start | bytes 98312 | tf_op jit(solution)/shard_map/ppermute | solution.py:363
  119.5 1.3 collective-permute-done.2
  120.9 3.1 %collective-permute-start.3 = (bf16[128,128]{1,0:T(8,128)(2,1)S(1)}, bf16[128,128]{1,0:T(8,128)(2,1)S(1)}, u32[]{:S(2)}, u32[]{:S(2)}) collective-permute-start(bf16[128,128]{1,0:T(8,128)(2,1)S(1)} %add_convert_fusion.2), channel_id=1, source_target_pairs={{0,2},{1,3},{2,0},{3,1},{4,6},{5,7},{6,4},{7,5},{8,10},{9,11},{10,... | collective-permute-start | bytes 98312 | tf_op jit(solution)/shard_map/ppermute | solution.py:363
  123.9 5.2 %all-to-all-start.3 = ((bf16[32,32,256]{2,1,0:T(8,128)(2,1)}), bf16[32,32,256]{2,1,0:T(8,128)(2,1)S(1)}, u32[]{:S(2)}, u32[]{:S(2)}) async-start(bf16[32,32,256]{2,1,0:T(8,128)(2,1)} %add_convert_fusion), calls=%async_computation.3 | async-start | bytes 1048576 | tf_op jit(solution)/shard_map/all_to_all | solution.py:359
  129.1 0.0 collective-permute-done.3
  129.2 5.2 %collective-permute-start.4 = (bf16[128,128]{1,0:T(8,128)(2,1)S(1)}, bf16[128,128]{1,0:T(8,128)(2,1)S(1)}, u32[]{:S(2)}, u32[]{:S(2)}) collective-permute-start(bf16[128,128]{1,0:T(8,128)(2,1)S(1)} %add_convert_fusion.1), channel_id=1, source_target_pairs={{0,4},{1,5},{2,6},{3,7},{4,0},{5,1},{6,2},{7,3},{8,12},{9,13},{10,... | collective-permute-start | bytes 98312 | tf_op jit(solution)/shard_map/ppermute | solution.py:363
  134.4 1.6 %collective-permute-done.4 = bf16[128,128]{1,0:T(8,128)(2,1)S(1)} collective-permute-done((bf16[128,128]{1,0:T(8,128)(2,1)S(1)}, bf16[128,128]{1,0:T(8,128)(2,1)S(1)}, u32[]{:S(2)}, u32[]{:S(2)}) %collective-permute-start.4) | collective-permute-done | bytes 32800 | tf_op jit(solution)/shard_map/ppermute | solution.py:363
  135.9 0.6 fusion
  136.6 4.2 %all-to-all-done.3.z_ref = bf16[32,32,256]{2,1,0:T(8,128)(2,1)S(1)} async-done(((bf16[32,32,256]{2,1,0:T(8,128)(2,1)}), bf16[32,32,256]{2,1,0:T(8,128)(2,1)S(1)}, u32[]{:S(2)}, u32[]{:S(2)}) %all-to-all-start.3) | async-done | bytes 524320 | tf_op jit(solution)/shard_map/all_to_all | solution.py:359
  140.7 0.9 key_sums.1
  (6 shorter events, 0.1 us)
Async XLA Ops:
  0.6 77.2 %copy-start = (bf16[4096,64]{0,1:T(8,128)(2,1)S(1)}, bf16[4096,64]{0,1:T(8,128)(2,1)}, u32[]{:S(2)}) copy-start(bf16[4096,64]{0,1:T(8,128)(2,1)} %param.16) | copy-start | bytes 1572868
  5.0 42.5 %all-to-all-start = ((bf16[32,320,128]{2,1,0:T(8,128)(2,1)}), bf16[32,320,128]{2,1,0:T(8,128)(2,1)S(1)}, u32[]{:S(2)}, u32[]{:S(2)}) async-start(bf16[32,320,128]{2,1,0:T(8,128)(2,1)} %prepare.1), calls=%async_computation | async-start | bytes 5242880 | tf_op jit(solution)/shard_map/all_to_all | solution.py:359
  13.6 34.9 %copy-start.3 = (f32[64]{0:T(128)S(1)}, f32[64]{0:T(128)}, u32[]{:S(2)}) copy-start(f32[64]{0:T(128)} %constant.21) | copy-start | bytes 772
  47.5 6.0 %collective-permute-start = (bf16[32,64,128]{2,1,0:T(8,128)(2,1)S(1)}, bf16[32,64,128]{2,1,0:T(8,128)(2,1)S(1)}, u32[]{:S(2)}, u32[]{:S(2)}) collective-permute-start(bf16[32,64,128]{2,1,0:T(8,128)(2,1)S(1)} %keys_of.1), channel_id=1, source_target_pairs={{0,8},{8,0},{16,24},{24,16},{32,40},{40,32},{48,56},{56,48},{64,72... | collective-permute-start | bytes 1572872 | tf_op jit(solution)/shard_map/ppermute | solution.py:363
  73.9 20.8 %copy-start.1 = (bf16[2,64,4096]{2,1,0:T(8,128)(2,1)S(1)}, bf16[2,64,4096]{2,1,0:T(8,128)(2,1)}, u32[]{:S(2)}) copy-start(bf16[2,64,4096]{2,1,0:T(8,128)(2,1)} %hid_ref.1) | copy-start | bytes 3145732
  73.9 20.8 %copy-start.2 = (bf16[64,4096]{1,0:T(8,128)(2,1)S(1)}, bf16[64,4096]{1,0:T(8,128)(2,1)}, u32[]{:S(2)}) copy-start(bf16[64,4096]{1,0:T(8,128)(2,1)} %up_ref.1) | copy-start | bytes 1572868
  73.9 20.8 %all-to-all-start.1 = ((bf16[32,64,256]{2,1,0:T(8,128)(2,1)}), bf16[32,64,256]{2,1,0:T(8,128)(2,1)S(1)}, u32[]{:S(2)}, u32[]{:S(2)}) async-start(bf16[32,64,256]{2,1,0:T(8,128)(2,1)} %bitcast.7), calls=%async_computation.1 | async-start | bytes 2097152 | tf_op jit(solution)/shard_map/all_to_all | solution.py:359
  96.8 20.8 %all-to-all-start.2 = ((bf16[32,128,128]{2,1,0:T(8,128)(2,1)}), bf16[32,128,128]{2,1,0:T(8,128)(2,1)S(1)}, u32[]{:S(2)}, u32[]{:S(2)}) async-start(bf16[32,128,128]{2,1,0:T(8,128)(2,1)} %get-tuple-element.18), calls=%async_computation.2 | async-start | bytes 2097152 | tf_op jit(solution)/shard_map/all_to_all | solution.py:359
  100.8 2.4 %collective-permute-start.1 = (bf16[32,32,256]{2,1,0:T(8,128)(2,1)}, bf16[32,32,256]{2,1,0:T(8,128)(2,1)S(1)}, u32[]{:S(2)}, u32[]{:S(2)}) collective-permute-start(bf16[32,32,256]{2,1,0:T(8,128)(2,1)} %get-tuple-element.17), channel_id=1, source_target_pairs={{0,8},{8,0},{16,24},{24,16},{32,40},{40,32},{48,56},{56,48},{64,72... | collective-permute-start | bytes 1572872 | tf_op jit(solution)/shard_map/ppermute | solution.py:363
  117.8 3.0 %collective-permute-start.2 = (bf16[128,128]{1,0:T(8,128)(2,1)S(1)}, bf16[128,128]{1,0:T(8,128)(2,1)S(1)}, u32[]{:S(2)}, u32[]{:S(2)}) collective-permute-start(bf16[128,128]{1,0:T(8,128)(2,1)S(1)} %reduce_sum.12), channel_id=1, source_target_pairs={{0,1},{1,0},{2,3},{3,2},{4,5},{5,4},{6,7},{7,6},{8,9},{9,8},{10,11... | collective-permute-start | bytes 98312 | tf_op jit(solution)/shard_map/ppermute | solution.py:363
  120.9 8.3 %collective-permute-start.3 = (bf16[128,128]{1,0:T(8,128)(2,1)S(1)}, bf16[128,128]{1,0:T(8,128)(2,1)S(1)}, u32[]{:S(2)}, u32[]{:S(2)}) collective-permute-start(bf16[128,128]{1,0:T(8,128)(2,1)S(1)} %add_convert_fusion.2), channel_id=1, source_target_pairs={{0,2},{1,3},{2,0},{3,1},{4,6},{5,7},{6,4},{7,5},{8,10},{9,11},{10,... | collective-permute-start | bytes 98312 | tf_op jit(solution)/shard_map/ppermute | solution.py:363
  123.9 16.8 %all-to-all-start.3 = ((bf16[32,32,256]{2,1,0:T(8,128)(2,1)}), bf16[32,32,256]{2,1,0:T(8,128)(2,1)S(1)}, u32[]{:S(2)}, u32[]{:S(2)}) async-start(bf16[32,32,256]{2,1,0:T(8,128)(2,1)} %add_convert_fusion), calls=%async_computation.3 | async-start | bytes 1048576 | tf_op jit(solution)/shard_map/all_to_all | solution.py:359
  129.2 6.8 %collective-permute-start.4 = (bf16[128,128]{1,0:T(8,128)(2,1)S(1)}, bf16[128,128]{1,0:T(8,128)(2,1)S(1)}, u32[]{:S(2)}, u32[]{:S(2)}) collective-permute-start(bf16[128,128]{1,0:T(8,128)(2,1)S(1)} %add_convert_fusion.1), channel_id=1, source_target_pairs={{0,4},{1,5},{2,6},{3,7},{4,0},{5,1},{6,2},{7,3},{8,12},{9,13},{10,... | collective-permute-start | bytes 98312 | tf_op jit(solution)/shard_map/ppermute | solution.py:363
